TPU v7x, 32 devices: a whole 2x2x4 slice. The times are simulated.
32 devices in a mesh: row: 4 (over y, x), col: 8 (over z, core).
Axes of the slice: x: 2, y: 2, z: 4, core: 2. Of those that a mesh axis runs over, the one named last changes fastest.
Arguments:
- view_a: bfloat16 [3072, 8192], P(('row', 'col')), may hold values from -1000 to 1000
- view_b: bfloat16 [3072, 8192], P(('row', 'col')), may hold values from -1000 to 1000
Outputs:
- correlation: float32 [8192, 8192], P('row', 'col')
- loss: float32 [], replicated
All inputs are finite; a program needn't handle non-finite values.
Results may differ from a plain program's by a relative error of at most 0.0013.
Values may be sent and summed in bfloat16 or wider, within the bound.
A program may use at most 192 MiB of HBM per device.

v0:
```python
import jax
import jax.numpy as jnp
from jax import lax
from jax.sharding import PartitionSpec as P


def moments(view):
    values = view.astype(jnp.float32)
    return (jnp.sum(values, 0), jnp.sum(values * values, 0))


def scaled(view, total, squares, count):
    mean = total / count
    var = squares / count - mean * mean
    return ((view.astype(jnp.float32) - mean) * lax.rsqrt(var + 1e-05)).astype(jnp.bfloat16)


def shards(view_a, view_b):
    rows_local = view_a.shape[0]
    width = view_a.shape[1]
    n_row = lax.axis_size("row")
    n_col = lax.axis_size("col")
    count = rows_local * n_row * n_col
    left = lax.all_to_all(view_a, "row", split_axis=1, concat_axis=0, tiled=True)
    right = lax.all_to_all(view_b, "col", split_axis=1, concat_axis=0, tiled=True)
    part_total, part_squares = moments(left)
    part_total, part_squares = lax.psum((part_total, part_squares), "col")
    left = scaled(left, part_total, part_squares, count)
    side_total, side_squares = moments(right)
    side_total, side_squares = lax.psum((side_total, side_squares), "row")
    right = scaled(right, side_total, side_squares, count)
    row_block = left.shape[1]
    col_block = right.shape[1]
    every_left = lax.all_gather(left, "col", axis=0, tiled=True)
    grouped = every_left.reshape(n_col, n_row, rows_local, row_block)
    piece = lax.all_gather(right, "row", axis=0, tiled=True)
    groups = piece.shape[0] // right.shape[0]
    blocks = piece.reshape(groups, n_col, rows_local, col_block)
    product = jnp.einsum("ckbf,kcbg->fg", grouped, blocks, preferred_element_type=jnp.float32)
    correlation = product / count
    row_ids = lax.axis_index("row") * row_block + lax.broadcasted_iota(jnp.int32, (row_block, 1), 0)
    col_ids = lax.axis_index("col") * col_block + lax.broadcasted_iota(jnp.int32, (1, col_block), 1)
    on_diag = row_ids == col_ids
    squared = correlation * correlation
    diag_terms = jnp.where(on_diag, (1.0 - correlation) ** 2 - 0.0051 * squared, 0.0)
    partial_loss = 0.0051 * jnp.sum(squared) + jnp.sum(diag_terms)
    loss = lax.psum(partial_loss, ("row", "col")) / width
    return (correlation, loss)


def solution(mesh):
    return jax.shard_map(
        shards,
        mesh=mesh,
        in_specs=(P(("row", "col"), None), P(("row", "col"), None)),
        out_specs=(P("row", "col"), P()),
        check_vma=False,
    )
```

profile of v0, /device:TPU:0, one launch (start us, length us, event | category | flops | bytes accessed | tf_op | source)
XLA Modules:
  0.0 330.3 jit_solution(2563064573535867003)
XLA Ops:
  7.2 0.0 all-gather.5.cloned.1.call-start
  7.2 1.5 copy.26
  8.8 43.9 %all_to_all.26 = bf16[96,8,1024]{2,0,1:T(8,128)(2,1)S(1)} all-to-all(bf16[96,8,1024]{2,0,1:T(8,128)(2,1)S(1)} %bitcast.31), channel_id=1, replica_groups=mesh['row'=4,'col'=8] {'col'}, dimensions={1} | all-to-all | bytes 3145728 | tf_op jit(solution)/shard_map/all_to_all | solution.py:25
  52.7 0.0 copy-start
  52.7 0.5 convert_reduce_fusion
  53.2 10.1 %all-reduce.1 = (f32[1024]{0:T(1024)S(1)}, f32[1024]{0:T(1024)S(1)}) all-reduce(f32[1024]{0:T(1024)S(1)} %get-tuple-element.5, f32[1024]{0:T(1024)S(1)} %get-tuple-element.4), channel_id=1, replica_groups=mesh['row'=4,'col'=8] {'row'}, use_global_device_ids=true, to_apply=%region_7.0 | all-reduce | flops 2048 | bytes 16384 | tf_op jit(solution)/shard_map/psum | solution.py:30
  63.3 1.6 fusion.5
  64.9 0.0 all-gather.5.cloned.1.call-update
  64.9 0.0 all-gather.3.cloned.1.call-start
  64.9 0.0 copy-done
  64.9 0.2 copy.27
  65.1 34.5 %all_to_all.27 = bf16[96,4,2048]{2,0,1:T(8,128)(2,1)S(1)} all-to-all(bf16[96,4,2048]{2,0,1:T(8,128)(2,1)S(1)} %bitcast.32), channel_id=1, replica_groups=mesh['row'=4,'col'=8] {'row'}, dimensions={1} | all-to-all | bytes 3145728 | tf_op jit(solution)/shard_map/all_to_all | solution.py:24
  99.6 0.4 convert_reduce_fusion.1
  100.1 25.9 %all-reduce = (f32[2048]{0:T(1024)S(1)}, f32[2048]{0:T(1024)S(1)}) all-reduce(f32[2048]{0:T(1024)S(1)} %get-tuple-element.7, f32[2048]{0:T(1024)S(1)} %get-tuple-element.6), channel_id=1, replica_groups=mesh['row'=4,'col'=8] {'col'}, use_global_device_ids=true, to_apply=%region_3.0 | all-reduce | flops 4096 | bytes 32768 | tf_op jit(solution)/shard_map/psum | solution.py:27
  126.0 1.6 fusion.7
  127.6 0.0 all-gather.3.cloned.1.call-update
  127.6 14.1 %all-gather.5.cloned.1.call-done = bf16[3072,1024]{1,0:T(8,128)(2,1)} async-done(((bf16[768,1024]{1,0:T(8,128)(2,1)}), bf16[3072,1024]{1,0:T(8,128)(2,1)}) %all-gather.5.cloned.1.call-update) | async-done | bytes 6291472 | tf_op jit(solution)/shard_map/all_gather | solution.py:36
  141.7 119.0 %all-gather.3.cloned.1.call-done = bf16[3072,2048]{1,0:T(8,128)(2,1)} async-done(((bf16[384,2048]{1,0:T(8,128)(2,1)}), bf16[3072,2048]{1,0:T(8,128)(2,1)}) %all-gather.3.cloned.1.call-update) | async-done | bytes 12582928 | tf_op jit(solution)/shard_map/all_gather | solution.py:34
  260.6 21.4 %select_reduce_fusion = (f32[]{:T(128)}, f32[]{:T(128)}, f32[2048,1024]{1,0:T(8,128)}) fusion(s32[1024]{0:T(1024)S(1)} %iota_add_fusion.1, s32[2048]{0:T(1024)S(1)} %iota_add_fusion, bf16[8,4,96,2048]{3,2,1,0:T(8,128)(2,1)} %bitcast.35, bf16[4,8,96,1024]{3,2,1,0:T(8,128)(2,1)} %bitcast.36), kind=kOutput, calls=%fused_computation.1 | convolution fusion | flops 12905873408 | bytes 27275272 | tf_op jit(solution)/shard_map/ckbf,kcbg->fg/dot_general | solution.py:39
  283.3 38.4 %psum.39 = f32[]{:T(128)} all-reduce(f32[]{:T(128)S(6)} %add.55), channel_id=1, replica_groups=mesh['row'=4,'col'=8] {'row','col'}, use_global_device_ids=true, to_apply=%region_10.11 | all-reduce | flops 1 | bytes 8 | tf_op jit(solution)/shard_map/psum | solution.py:47
  (4 shorter events, 0.0 us)
Async XLA Ops:
  7.2 134.5 %all-gather.5.cloned.1.call-start = ((), (), s32[]{:S(2)}) async-start(), calls=%async_computation.3 | async-start | bytes 7864320 | tf_op jit(solution)/shard_map/all_gather | solution.py:36
  52.7 12.2 %copy-start = (bf16[96,8192]{1,0:T(8,128)(2,1)S(1)}, bf16[96,8192]{1,0:T(8,128)(2,1)}, u32[]{:S(2)}) copy-start(bf16[96,8192]{1,0:T(8,128)(2,1)} %param.2) | copy-start | bytes 4718596
  64.9 195.8 %all-gather.3.cloned.1.call-start = ((), (), s32[]{:S(2)}) async-start(), calls=%async_computation.2 | async-start | bytes 14155776 | tf_op jit(solution)/shard_map/all_gather | solution.py:34
Sparse Core Ops, SparseCore 0:
  65.0 76.6 all-gather.4
  143.9 116.6 all-gather.2
where the time goes:
time: 331 us; the launch traced here: 330 us
  blocking collectives  153 us (46%)
  waiting for transfers between devices  133 us (40%)
  matrix products  21.4 us (6%)
  between operations  17.1 us (5%)
  other arithmetic  4.09 us (1%)
    all_gather x1, waiting for transfers between devices, shards(): every_left = lax.all_gather(left, 'col', axis=0, tiled=True)  119 us
    all_to_all x1, blocking collectives, shards(): lax.all_to_all(view_b, 'col', split_axis=1, concat_axis=0, tiled=True)  43.9 us
    psum x1, blocking collectives, shards(): loss = lax.psum(partial_loss, ('row', 'col')) / width  38.4 us
    all_to_all x1, blocking collectives, shards(): lax.all_to_all(view_a, 'row', split_axis=1, concat_axis=0, tiled=True)  34.5 us
    psum x1, blocking collectives, shards(): part_total, part_squares = lax.psum((part_total, part_squares), 'col')  25.9 us
    dot_general x1, matrix products, shards(): jnp.einsum('ckbf,kcbg->fg', grouped, blocks, preferred_element_type=jnp.f...  21.4 us
    all_gather x1, waiting for transfers between devices, shards(): piece = lax.all_gather(right, 'row', axis=0, tiled=True)  14.1 us
    psum x1, blocking collectives, shards(): side_total, side_squares = lax.psum((side_total, side_squares), 'row')  10.1 us
  transfers between devices with their start and end apart: 2, of which 2 were waited for; matrix products, arithmetic and copies ran while one was open for 1% of the time, Pallas kernels for 0%

commit v1 on v0

v1 whole, which is shorter than its diff:
```python
import functools

import jax
import jax.numpy as jnp
from jax import lax
from jax.experimental import pallas as pl
from jax.experimental.pallas import tpu as pltpu
from jax.sharding import PartitionSpec as P

MESH = pl.DeviceIdType.MESH
F32 = jnp.float32
BF16 = jnp.bfloat16


def body(
    n_row, n_col, width,
    a_in, b_in, out, loss_out,
    a_all, b_all, nb, stat_a, stat_b, coef_a, coef_b, loss_row, loss_col,
    s_a, r_a, s_b, r_b, s_sa, r_sa, s_sb, r_sb, s_line, r_line, s_fwd, r_fwd,
    s_lr, r_lr, s_lc, r_lc, own_sem,
):
    t = a_in.shape[0]
    rb = a_in.shape[1] // n_row
    cb = b_in.shape[1] // n_col
    count = t * n_row * n_col
    n_z = n_col // 2
    r = lax.axis_index("row")
    c = lax.axis_index("col")
    z = c // 2
    k = c % 2
    mine = pl.ds(pl.multiple_of(r * t, t), t)

    def row_mate(i):
        return (r + i) % n_row

    def col_mate(j):
        return (c + j) % n_col

    def remote(src, dst, ss, rs, dev):
        return pltpu.make_async_remote_copy(
            src_ref=src, dst_ref=dst, send_sem=ss, recv_sem=rs, device_id=dev, device_id_type=MESH
        )

    barrier = pltpu.get_barrier_semaphore()
    for i in range(1, n_row):
        pl.semaphore_signal(barrier, inc=1, device_id=(row_mate(i), c), device_id_type=MESH)
    for j in range(1, n_col):
        pl.semaphore_signal(barrier, inc=1, device_id=(r, col_mate(j)), device_id_type=MESH)
    pl.semaphore_wait(barrier, n_row + n_col - 2)

    def send_a(i):
        dst = row_mate(i)
        cols = pl.ds(pl.multiple_of(dst * rb, rb), rb)
        return remote(a_in.at[:, cols], a_all.at[c, mine], s_a.at[i], r_a.at[i], (dst, c))

    def got_a(i):
        src = row_mate(n_row - i)
        rows = pl.ds(pl.multiple_of(src * t, t), t)
        return remote(a_all.at[c, rows], a_all.at[c, rows], s_a.at[i], r_a.at[i], (src, c))

    def send_b(j):
        dst = col_mate(j)
        cols = pl.ds(pl.multiple_of(dst * cb, cb), cb)
        return remote(b_in.at[:, cols], b_all.at[c, mine], s_b.at[j], r_b.at[j], (r, dst))

    def got_b(j):
        src = col_mate(n_col - j)
        return remote(b_all.at[src, mine], b_all.at[src, mine], s_b.at[j], r_b.at[j], (r, src))

    for i in range(1, n_row):
        send_a(i).start()
    for j in range(1, n_col):
        send_b(j).start()
    own_a = pltpu.make_async_copy(
        a_in.at[:, pl.ds(pl.multiple_of(r * rb, rb), rb)], a_all.at[c, mine], own_sem.at[0]
    )
    own_b = pltpu.make_async_copy(
        b_in.at[:, pl.ds(pl.multiple_of(c * cb, cb), cb)], b_all.at[c, mine], own_sem.at[1]
    )
    own_a.start()
    own_b.start()

    own_a.wait()
    for i in range(1, n_row):
        got_a(i).wait_recv()

    def moments_a(q, carry):
        cols = pl.ds(pl.multiple_of(q * 128, 128), 128)
        x = a_all[c, :, cols].astype(F32)
        stat_a[c, 0:1, cols] = jnp.sum(x, 0, keepdims=True)
        stat_a[c, 1:2, cols] = jnp.sum(x * x, 0, keepdims=True)
        return carry

    lax.fori_loop(0, rb // 128, moments_a, 0)

    def send_sa(j):
        return remote(stat_a.at[c], stat_a.at[c], s_sa.at[j], r_sa.at[j], (r, col_mate(j)))

    def got_sa(j):
        src = col_mate(n_col - j)
        return remote(stat_a.at[src], stat_a.at[src], s_sa.at[j], r_sa.at[j], (r, src))

    for j in range(1, n_col):
        send_sa(j).start()

    def line(way, chunk, p, dev_c):
        rows = pl.ds(pl.multiple_of(p * t, t), t)
        ref = a_all.at[chunk, rows]
        return remote(ref, ref, s_line.at[way, chunk, p], r_line.at[chunk, p], (r, dev_c))

    partner = z * 2 + (1 - k)

    def up(chunk, p):
        return line(0, chunk, p, lax.min(c + 2, n_col - 2 + k))

    def down(chunk, p):
        return line(1, chunk, p, lax.max(c - 2, k))

    def across(chunk, p):
        return line(2, chunk, p, partner)

    can_up = z < n_z - 1
    can_down = z > 0

    for p in range(n_row):
        @pl.when(can_up)
        def _():
            up(c, p).start()

        @pl.when(can_down)
        def _():
            down(c, p).start()

        across(c, p).start()

    own_b.wait()
    for j in range(1, n_col):
        got_b(j).wait_recv()

    def moments_b(q, carry):
        cols = pl.ds(pl.multiple_of(q * 128, 128), 128)
        total = jnp.zeros((1, 128), F32)
        squares = jnp.zeros((1, 128), F32)
        for g in range(n_col):
            x = b_all[g, mine, cols].astype(F32)
            total = total + jnp.sum(x, 0, keepdims=True)
            squares = squares + jnp.sum(x * x, 0, keepdims=True)
        stat_b[r, 0:1, cols] = total
        stat_b[r, 1:2, cols] = squares
        return carry

    lax.fori_loop(0, cb // 128, moments_b, 0)

    def send_sb(i):
        return remote(stat_b.at[r], stat_b.at[r], s_sb.at[i], r_sb.at[i], (row_mate(i), c))

    def got_sb(i):
        src = row_mate(n_row - i)
        return remote(stat_b.at[src], stat_b.at[src], s_sb.at[i], r_sb.at[i], (src, c))

    for i in range(1, n_row):
        send_sb(i).start()

    def send_fwd(i, g):
        return remote(b_all.at[g, mine], b_all.at[g, mine], s_fwd.at[i, g], r_fwd.at[i, g], (row_mate(i), c))

    def got_fwd(i, g):
        src = row_mate(n_row - i)
        rows = pl.ds(pl.multiple_of(src * t, t), t)
        return remote(b_all.at[g, rows], b_all.at[g, rows], s_fwd.at[i, g], r_fwd.at[i, g], (src, c))

    def each_chunk(d, do):
        for side in range(2):
            zz = z - d if side == 0 else z + d
            ok = (zz >= 0) if side == 0 else jnp.logical_and(zz < n_z, d > 0)

            @pl.when(ok)
            def _():
                do(zz * 2 + k, side)
                do(zz * 2 + (1 - k), side)

    def forward(d, carry):
        def do(g, side):
            for i in range(1, n_row):
                send_fwd(i, g).start()

        each_chunk(d, do)
        return carry

    lax.fori_loop(0, n_z, forward, 0)

    def clear(q, carry):
        rows = pl.ds(pl.multiple_of(q * 64, 64), 64)
        out[rows, :] = jnp.zeros((64, cb), F32)
        return carry

    lax.fori_loop(0, rb // 64, clear, 0)

    for j in range(1, n_col):
        got_sa(j).wait_recv()
    for i in range(1, n_row):
        got_sb(i).wait_recv()

    def coefs(stat, coef):
        sums = jnp.sum(stat[...], 0)
        mean = sums[0:1] / count
        var = sums[1:2] / count - mean * mean
        coef[0:1, :] = mean
        coef[1:2, :] = lax.rsqrt(var + 1e-05)

    coefs(stat_a, coef_a)
    coefs(stat_b, coef_b)

    tile = 256

    def process(g, side):
        for i in range(1, n_row):
            got_fwd(i, g).wait_recv()

        def norm_b(q, carry):
            cols = pl.ds(pl.multiple_of(q * 128, 128), 128)
            x = b_all[g, :, cols].astype(F32)
            nb[:, cols] = ((x - coef_b[0:1, cols]) * coef_b[1:2, cols]).astype(BF16)
            return carry

        lax.fori_loop(0, cb // 128, norm_b, 0)

        def mul(q, carry):
            cols = pl.ds(pl.multiple_of(q * tile, tile), tile)
            x = a_all[g, :, cols].astype(F32)
            na = ((x - coef_a[0:1, cols]) * coef_a[1:2, cols]).astype(BF16)
            out[cols, :] += lax.dot_general(
                na, nb[...], (((0,), (0,)), ((), ())), preferred_element_type=F32
            )
            return carry

        lax.fori_loop(0, rb // tile, mul, 0)

    def process_all(d):
        def one(q, carry):
            side = q // 2
            zz = jnp.where(side == 0, z - d, z + d)
            ok = jnp.logical_and(zz >= 0, zz < n_z)
            ok = jnp.logical_and(ok, jnp.logical_or(side == 0, d > 0))
            other = q % 2
            g = zz * 2 + jnp.where(other == 0, k, 1 - k)

            @pl.when(ok)
            def _():
                @pl.when(other == 1)
                def _():
                    for p in range(n_row):
                        across(g, p).wait_recv()

                process(g, 0)

            return carry

        lax.fori_loop(0, 4, one, 0)

    def step(d, carry):
        from_low = z - d >= 0
        from_high = z + d < n_z
        low = (z - d) * 2 + k
        high = (z + d) * 2 + k
        for p in range(n_row):
            @pl.when(from_low)
            def _():
                up(low, p).wait_recv()

                @pl.when(can_up)
                def _():
                    up(low, p).start()

                across(low, p).start()

            @pl.when(from_high)
            def _():
                down(high, p).wait_recv()

                @pl.when(can_down)
                def _():
                    down(high, p).start()

                across(high, p).start()

        process_all(d - 1)
        return carry

    lax.fori_loop(1, n_z, step, 0)
    process_all(n_z - 1)

    def part(q, carry):
        rows = pl.ds(pl.multiple_of(q * 8, 8), 8)
        x = out[rows, :] / count
        row_ids = r * rb + q * 8 + lax.broadcasted_iota(jnp.int32, (8, cb), 0)
        col_ids = c * cb + lax.broadcasted_iota(jnp.int32, (8, cb), 1)
        sq = x * x
        return carry + jnp.where(row_ids == col_ids, (1.0 - x) * (1.0 - x), 0.0051 * sq)

    share = lax.fori_loop(0, rb // 8, part, jnp.zeros((8, cb), F32), unroll=4)
    folded = share[:, 0:128]
    for q in range(1, cb // 128):
        folded = folded + share[:, q * 128 : (q + 1) * 128]
    loss_row[r] = folded

    def send_lr(i):
        return remote(loss_row.at[r], loss_row.at[r], s_lr.at[i], r_lr.at[i], (row_mate(i), c))

    def got_lr(i):
        src = row_mate(n_row - i)
        return remote(loss_row.at[src], loss_row.at[src], s_lr.at[i], r_lr.at[i], (src, c))

    def send_lc(j):
        return remote(loss_col.at[c], loss_col.at[c], s_lc.at[j], r_lc.at[j], (r, col_mate(j)))

    def got_lc(j):
        src = col_mate(n_col - j)
        return remote(loss_col.at[src], loss_col.at[src], s_lc.at[j], r_lc.at[j], (r, src))

    for i in range(1, n_row):
        send_lr(i).start()
    for i in range(1, n_row):
        got_lr(i).wait_recv()
    loss_col[c] = jnp.sum(loss_row[...], 0)
    for j in range(1, n_col):
        send_lc(j).start()

    for i in range(1, n_row):
        send_a(i).wait_send()
        send_sb(i).wait_send()
        send_lr(i).wait_send()
    for j in range(1, n_col):
        send_b(j).wait_send()
        send_sa(j).wait_send()

    def drain(g, carry):
        for i in range(1, n_row):
            send_fwd(i, g).wait_send()
        zz = g // 2
        for p in range(n_row):
            @pl.when(g % 2 == k)
            def _():
                @pl.when(jnp.logical_and(zz <= z, can_up))
                def _():
                    up(g, p).wait_send()

                @pl.when(jnp.logical_and(zz >= z, can_down))
                def _():
                    down(g, p).wait_send()

                across(g, p).wait_send()

        return carry

    lax.fori_loop(0, n_col, drain, 0)

    for j in range(1, n_col):
        got_lc(j).wait_recv()
    loss_out[...] = jnp.broadcast_to(
        jnp.sum(jnp.sum(loss_col[...], 0), keepdims=True) / width, loss_out.shape
    )
    for j in range(1, n_col):
        send_lc(j).wait_send()


def shards(view_a, view_b):
    t, width = view_a.shape
    n_row = lax.axis_size("row")
    n_col = lax.axis_size("col")
    rb = width // n_row
    cb = width // n_col
    count = t * n_row * n_col
    n_chunk = t * n_row
    dma = pltpu.SemaphoreType.DMA
    size = 2 * (count * (rb + cb) + n_chunk * cb + 2 * t * width) + 4 * rb * cb
    product, loss = pl.pallas_call(
        functools.partial(body, n_row, n_col, width),
        out_shape=(
            jax.ShapeDtypeStruct((rb, cb), F32),
            jax.ShapeDtypeStruct((8, 128), F32),
        ),
        in_specs=[pl.BlockSpec(memory_space=pltpu.VMEM)] * 2,
        out_specs=(pl.BlockSpec(memory_space=pltpu.VMEM),) * 2,
        scratch_shapes=[
            pltpu.VMEM((n_col, n_chunk, rb), BF16),
            pltpu.VMEM((n_col, n_chunk, cb), BF16),
            pltpu.VMEM((n_chunk, cb), BF16),
            pltpu.VMEM((n_col, 2, rb), F32),
            pltpu.VMEM((n_row, 2, cb), F32),
            pltpu.VMEM((2, rb), F32),
            pltpu.VMEM((2, cb), F32),
            pltpu.VMEM((n_row, 8, 128), F32),
            pltpu.VMEM((n_col, 8, 128), F32),
            dma((n_row,)), dma((n_row,)),
            dma((n_col,)), dma((n_col,)),
            dma((n_col,)), dma((n_col,)),
            dma((n_row,)), dma((n_row,)),
            dma((3, n_col, n_row)), dma((n_col, n_row)),
            dma((n_row, n_col)), dma((n_row, n_col)),
            dma((n_row,)), dma((n_row,)),
            dma((n_col,)), dma((n_col,)),
            dma((2,)),
        ],
        compiler_params=pltpu.CompilerParams(
            collective_id=0, has_side_effects=True, vmem_limit_bytes=size + (4 << 20)
        ),
        name="twins",
    )(view_a, view_b)
    return product / count, loss[0, 0]


def solution(mesh):
    return jax.shard_map(
        shards,
        mesh=mesh,
        in_specs=(P(("row", "col"), None), P(("row", "col"), None)),
        out_specs=(P("row", "col"), P()),
        check_vma=False,
    )
```

time: 331 us -> 181 us (0.55)
  Pallas kernels: 0 us -> 173 us
  blocking collectives: 153 us -> 0 us
  waiting for transfers between devices: 133 us -> 0 us
  matrix products: 21.4 us -> 0 us
  between operations: 17.1 us -> 0.65 us
    pallas_call x0 -> x1, Pallas kernels: none -> 173 us  [shards(): pl.pallas_call(functools.partial(body, n_row, n_col, width), out_shape=(j...]
    all_gather x2 -> x0, waiting for transfers between devices: 133 us -> none  [the longest x1 119 us: shards(): every_left = lax.all_gather(left, 'col', axis=0, tiled=True)]
    all_to_all x2 -> x0, blocking collectives: 78.5 us -> none  [the longest x1 43.9 us: shards(): lax.all_to_all(view_b, 'col', split_axis=1, concat_axis=0, tiled=True)]
    psum x3 -> x0, blocking collectives: 74.4 us -> none  [the longest x1 38.4 us: shards(): loss = lax.psum(partial_loss, ('row', 'col')) / width]
    dot_general x1 -> x0, matrix products: 21.4 us -> none  [shards(): jnp.einsum('ckbf,kcbg->fg', grouped, blocks, preferred_element_type=jnp.f...]
    div x2 -> x1, other arithmetic: 0.02 us -> 4.44 us  [shards(): return (product / count, loss[0, 0])]
  transfers between devices with their start and end apart: 2 -> 0, of which waited for: 2 -> 0; matrix products, arithmetic and copies ran while one was open for 1% -> 0% of each run, Pallas kernels for 0% -> 0%
where the time goes in v1:
time: 181 us
  Pallas kernels  173 us (96%)
  other arithmetic  4.44 us (2%)
  local copies, waits for them, and re-layouts  3.32 us (2%)
    pallas_call x1, Pallas kernels, shards(): pl.pallas_call(functools.partial(body, n_row, n_col, width), out_shape=(j...  173 us
    div x1, other arithmetic, shards(): return (product / count, loss[0, 0])  4.44 us

profile of v1, /device:TPU:0, one launch (start us, length us, event | category | flops | bytes accessed | tf_op | source)
XLA Modules:
  0.0 181.2 jit_solution(2798455225249094868)
XLA Ops:
  0.6 0.0 copy-start
  0.6 1.4 copy-done
  2.0 0.0 copy-start.1
  2.0 1.4 copy-done.1
  3.4 172.8 %twins.1 = (f32[2048,1024]{1,0:T(8,128)S(1)}, f32[8,128]{1,0:T(8,128)S(1)}) custom-call(bf16[96,8192]{1,0:T(8,128)(2,1)S(1)} %copy-done, bf16[96,8192]{1,0:T(8,128)(2,1)S(1)} %copy-done.1), custom_call_target="tpu_custom_call" | custom-call | tf_op jit(solution)/shard_map/twins/pallas_call | solution.py:377
  176.3 0.5 slice.3
  176.8 4.4 %broadcast_multiply_fusion = f32[2048,1024]{1,0:T(8,128)} fusion(f32[2048,1024]{1,0:T(8,128)S(1)} %get-tuple-element.4), kind=kLoop, calls=%fused_computation | loop fusion | flops 2097152 | bytes 16777216 | tf_op jit(solution)/shard_map/div | solution.py:410
Async XLA Ops:
  0.6 1.4 copy-start
  2.0 1.4 copy-start.1

commit v2 on v1

--- a/solution.py
+++ b/solution.py
@@ -41,36 +41,6 @@
             src_ref=src, dst_ref=dst, send_sem=ss, recv_sem=rs, device_id=dev, device_id_type=MESH
         )
 
-    barrier = pltpu.get_barrier_semaphore()
-    for i in range(1, n_row):
-        pl.semaphore_signal(barrier, inc=1, device_id=(row_mate(i), c), device_id_type=MESH)
-    for j in range(1, n_col):
-        pl.semaphore_signal(barrier, inc=1, device_id=(r, col_mate(j)), device_id_type=MESH)
-    pl.semaphore_wait(barrier, n_row + n_col - 2)
-
-    def send_a(i):
-        dst = row_mate(i)
-        cols = pl.ds(pl.multiple_of(dst * rb, rb), rb)
-        return remote(a_in.at[:, cols], a_all.at[c, mine], s_a.at[i], r_a.at[i], (dst, c))
-
-    def got_a(i):
-        src = row_mate(n_row - i)
-        rows = pl.ds(pl.multiple_of(src * t, t), t)
-        return remote(a_all.at[c, rows], a_all.at[c, rows], s_a.at[i], r_a.at[i], (src, c))
-
-    def send_b(j):
-        dst = col_mate(j)
-        cols = pl.ds(pl.multiple_of(dst * cb, cb), cb)
-        return remote(b_in.at[:, cols], b_all.at[c, mine], s_b.at[j], r_b.at[j], (r, dst))
-
-    def got_b(j):
-        src = col_mate(n_col - j)
-        return remote(b_all.at[src, mine], b_all.at[src, mine], s_b.at[j], r_b.at[j], (r, src))
-
-    for i in range(1, n_row):
-        send_a(i).start()
-    for j in range(1, n_col):
-        send_b(j).start()
     own_a = pltpu.make_async_copy(
         a_in.at[:, pl.ds(pl.multiple_of(r * rb, rb), rb)], a_all.at[c, mine], own_sem.at[0]
     )
@@ -80,9 +50,88 @@
     own_a.start()
     own_b.start()
 
+    barrier = pltpu.get_barrier_semaphore()
+    for i in range(1, n_row):
+        pl.semaphore_signal(barrier, inc=1, device_id=(row_mate(i), c), device_id_type=MESH)
+    for j in range(1, n_col):
+        pl.semaphore_signal(barrier, inc=1, device_id=(r, col_mate(j)), device_id_type=MESH)
+    pl.semaphore_wait(barrier, n_row + n_col - 2)
+
+    def send_a(i):
+        dst = row_mate(i)
+        cols = pl.ds(pl.multiple_of(dst * rb, rb), rb)
+        return remote(a_in.at[:, cols], a_all.at[c, mine], s_a.at[i], r_a.at[i], (dst, c))
+
+    def got_a(i):
+        src = row_mate(n_row - i)
+        rows = pl.ds(pl.multiple_of(src * t, t), t)
+        return remote(a_all.at[c, rows], a_all.at[c, rows], s_a.at[i], r_a.at[i], (src, c))
+
+    def send_b(j):
+        dst = col_mate(j)
+        cols = pl.ds(pl.multiple_of(dst * cb, cb), cb)
+        return remote(b_in.at[:, cols], b_all.at[c, mine], s_b.at[j], r_b.at[j], (r, dst))
+
+    def got_b(j):
+        src = col_mate(n_col - j)
+        return remote(b_all.at[src, mine], b_all.at[src, mine], s_b.at[j], r_b.at[j], (r, src))
+
+    for i in range(1, n_row):
+        send_a(i).start()
+
+    def line(way, chunk, p, dev_c):
+        rows = pl.ds(pl.multiple_of(p * t, t), t)
+        ref = a_all.at[chunk, rows]
+        return remote(ref, ref, s_line.at[way, chunk, p], r_line.at[chunk, p], (r, dev_c))
+
+    partner = z * 2 + (1 - k)
+
+    def up(chunk, p):
+        return line(0, chunk, p, lax.min(c + 2, n_col - 2 + k))
+
+    def down(chunk, p):
+        return line(1, chunk, p, lax.max(c - 2, k))
+
+    def across(chunk, p):
+        return line(2, chunk, p, partner)
+
+    can_up = z < n_z - 1
+    can_down = z > 0
+
+    def slice_at(o):
+        return (r + n_row - o) % n_row
+
+    def send_line(o):
+        p = slice_at(o)
+
+        @pl.when(can_up)
+        def _():
+            up(c, p).start()
+
+        @pl.when(can_down)
+        def _():
+            down(c, p).start()
+
+        across(c, p).start()
+
     own_a.wait()
-    for i in range(1, n_row):
-        got_a(i).wait_recv()
+    send_line(0)
+
+    for dist in range(n_z - 1, 0, -1):
+        for side in range(2):
+            zz = z - dist if side == 0 else z + dist
+
+            @pl.when(jnp.logical_and(zz >= 0, zz < n_z))
+            def _():
+                for other in range(2):
+                    send_b((zz * 2 + (k + other) % 2 + n_col - c) % n_col).start()
+
+    send_b((partner + n_col - c) % n_col).start()
+
+    for o in range(1, n_row):
+        got_a(o).wait_recv()
+        if o < n_row - 1:
+            send_line(o)
 
     def moments_a(q, carry):
         cols = pl.ds(pl.multiple_of(q * 128, 128), 128)
@@ -102,40 +151,44 @@
 
     for j in range(1, n_col):
         send_sa(j).start()
-
-    def line(way, chunk, p, dev_c):
-        rows = pl.ds(pl.multiple_of(p * t, t), t)
-        ref = a_all.at[chunk, rows]
-        return remote(ref, ref, s_line.at[way, chunk, p], r_line.at[chunk, p], (r, dev_c))
-
-    partner = z * 2 + (1 - k)
-
-    def up(chunk, p):
-        return line(0, chunk, p, lax.min(c + 2, n_col - 2 + k))
-
-    def down(chunk, p):
-        return line(1, chunk, p, lax.max(c - 2, k))
-
-    def across(chunk, p):
-        return line(2, chunk, p, partner)
-
-    can_up = z < n_z - 1
-    can_down = z > 0
-
-    for p in range(n_row):
-        @pl.when(can_up)
+    if n_row > 1:
+        send_line(n_row - 1)
+
+    def send_fwd(i, g):
+        return remote(b_all.at[g, mine], b_all.at[g, mine], s_fwd.at[i, g], r_fwd.at[i, g], (row_mate(i), c))
+
+    def got_fwd(i, g):
+        src = row_mate(n_row - i)
+        rows = pl.ds(pl.multiple_of(src * t, t), t)
+        return remote(b_all.at[g, rows], b_all.at[g, rows], s_fwd.at[i, g], r_fwd.at[i, g], (src, c))
+
+    def each_chunk(d, do):
+        for side in range(2):
+            zz = z - d if side == 0 else z + d
+            ok = (zz >= 0) if side == 0 else jnp.logical_and(zz < n_z, d > 0)
+
+            @pl.when(ok)
+            def _():
+                do(zz * 2 + k, side)
+                do(zz * 2 + (1 - k), side)
+
+    def forward(d, carry):
+        def do(g, side):
+            for i in range(1, n_row):
+                send_fwd(i, g).start()
+
+        each_chunk(d, do)
+        return carry
+
+    own_b.wait()
+    near = 1 + (n_col - 2) * (1 - k)
+    got_b(near).wait_recv()
+    forward(0, 0)
+    for j in range(1, n_col):
+        @pl.when(j != near)
         def _():
-            up(c, p).start()
-
-        @pl.when(can_down)
-        def _():
-            down(c, p).start()
-
-        across(c, p).start()
-
-    own_b.wait()
-    for j in range(1, n_col):
-        got_b(j).wait_recv()
+            got_b(j).wait_recv()
+
 
     def moments_b(q, carry):
         cols = pl.ds(pl.multiple_of(q * 128, 128), 128)
@@ -161,33 +214,7 @@
     for i in range(1, n_row):
         send_sb(i).start()
 
-    def send_fwd(i, g):
-        return remote(b_all.at[g, mine], b_all.at[g, mine], s_fwd.at[i, g], r_fwd.at[i, g], (row_mate(i), c))
-
-    def got_fwd(i, g):
-        src = row_mate(n_row - i)
-        rows = pl.ds(pl.multiple_of(src * t, t), t)
-        return remote(b_all.at[g, rows], b_all.at[g, rows], s_fwd.at[i, g], r_fwd.at[i, g], (src, c))
-
-    def each_chunk(d, do):
-        for side in range(2):
-            zz = z - d if side == 0 else z + d
-            ok = (zz >= 0) if side == 0 else jnp.logical_and(zz < n_z, d > 0)
-
-            @pl.when(ok)
-            def _():
-                do(zz * 2 + k, side)
-                do(zz * 2 + (1 - k), side)
-
-    def forward(d, carry):
-        def do(g, side):
-            for i in range(1, n_row):
-                send_fwd(i, g).start()
-
-        each_chunk(d, do)
-        return carry
-
-    lax.fori_loop(0, n_z, forward, 0)
+    lax.fori_loop(1, n_z, forward, 0)
 
     def clear(q, carry):
         rows = pl.ds(pl.multiple_of(q * 64, 64), 64)
@@ -211,15 +238,20 @@
     coefs(stat_a, coef_a)
     coefs(stat_b, coef_b)
 
-    tile = 256
-
-    def process(g, side):
-        for i in range(1, n_row):
-            got_fwd(i, g).wait_recv()
+    tile = min(1024, rb)
+    depth = 2 * n_row * t
+
+    def process(zz):
+        pair = pl.ds(zz * 2, 2)
+        for p in range(n_row):
+            across(zz * 2 + (1 - k), p).wait_recv()
+        for g in range(2):
+            for i in range(1, n_row):
+                got_fwd(i, zz * 2 + g).wait_recv()
 
         def norm_b(q, carry):
             cols = pl.ds(pl.multiple_of(q * 128, 128), 128)
-            x = b_all[g, :, cols].astype(F32)
+            x = b_all[pair, :, cols].astype(F32).reshape(depth, 128)
             nb[:, cols] = ((x - coef_b[0:1, cols]) * coef_b[1:2, cols]).astype(BF16)
             return carry
 
@@ -227,7 +259,7 @@
 
         def mul(q, carry):
             cols = pl.ds(pl.multiple_of(q * tile, tile), tile)
-            x = a_all[g, :, cols].astype(F32)
+            x = a_all[pair, :, cols].astype(F32).reshape(depth, tile)
             na = ((x - coef_a[0:1, cols]) * coef_a[1:2, cols]).astype(BF16)
             out[cols, :] += lax.dot_general(
                 na, nb[...], (((0,), (0,)), ((), ())), preferred_element_type=F32
@@ -237,33 +269,27 @@
         lax.fori_loop(0, rb // tile, mul, 0)
 
     def process_all(d):
-        def one(q, carry):
-            side = q // 2
+        def one(side, carry):
             zz = jnp.where(side == 0, z - d, z + d)
             ok = jnp.logical_and(zz >= 0, zz < n_z)
             ok = jnp.logical_and(ok, jnp.logical_or(side == 0, d > 0))
-            other = q % 2
-            g = zz * 2 + jnp.where(other == 0, k, 1 - k)
 
             @pl.when(ok)
             def _():
-                @pl.when(other == 1)
-                def _():
-                    for p in range(n_row):
-                        across(g, p).wait_recv()
-
-                process(g, 0)
+                process(zz)
 
             return carry
 
-        lax.fori_loop(0, 4, one, 0)
-
-    def step(d, carry):
+        lax.fori_loop(0, 2, one, 0)
+
+    def relay(d):
         from_low = z - d >= 0
         from_high = z + d < n_z
         low = (z - d) * 2 + k
         high = (z + d) * 2 + k
-        for p in range(n_row):
+        for o in range(n_row):
+            p = slice_at(o)
+
             @pl.when(from_low)
             def _():
                 up(low, p).wait_recv()
@@ -284,15 +310,24 @@
 
                 across(high, p).start()
 
-        process_all(d - 1)
-        return carry
-
-    lax.fori_loop(1, n_z, step, 0)
-    process_all(n_z - 1)
+    def step(d, carry):
+        @pl.when(d + 1 < n_z - 1)
+        def _():
+            relay(d + 1)
+
+        process_all(d)
+
+        @pl.when(d + 1 == n_z - 1)
+        def _():
+            relay(d + 1)
+
+        return carry
+
+    lax.fori_loop(0, n_z, step, 0)
 
     def part(q, carry):
         rows = pl.ds(pl.multiple_of(q * 8, 8), 8)
-        x = out[rows, :] / count
+        x = out[rows, :] * (1.0 / count)
         row_ids = r * rb + q * 8 + lax.broadcasted_iota(jnp.int32, (8, cb), 0)
         col_ids = c * cb + lax.broadcasted_iota(jnp.int32, (8, cb), 1)
         sq = x * x
@@ -373,19 +408,19 @@
     count = t * n_row * n_col
     n_chunk = t * n_row
     dma = pltpu.SemaphoreType.DMA
-    size = 2 * (count * (rb + cb) + n_chunk * cb + 2 * t * width) + 4 * rb * cb
+    size = 2 * (count * (rb + cb) + 2 * n_chunk * cb + 2 * t * width) + 4 * rb * cb
     product, loss = pl.pallas_call(
         functools.partial(body, n_row, n_col, width),
         out_shape=(
             jax.ShapeDtypeStruct((rb, cb), F32),
             jax.ShapeDtypeStruct((8, 128), F32),
         ),
-        in_specs=[pl.BlockSpec(memory_space=pltpu.VMEM)] * 2,
+        in_specs=[pl.BlockSpec(memory_space=pltpu.HBM)] * 2,
         out_specs=(pl.BlockSpec(memory_space=pltpu.VMEM),) * 2,
         scratch_shapes=[
             pltpu.VMEM((n_col, n_chunk, rb), BF16),
             pltpu.VMEM((n_col, n_chunk, cb), BF16),
-            pltpu.VMEM((n_chunk, cb), BF16),
+            pltpu.VMEM((2 * n_chunk, cb), BF16),
             pltpu.VMEM((n_col, 2, rb), F32),
             pltpu.VMEM((n_row, 2, cb), F32),
             pltpu.VMEM((2, rb), F32),
@@ -403,7 +438,7 @@
             dma((2,)),
         ],
         compiler_params=pltpu.CompilerParams(
-            collective_id=0, has_side_effects=True, vmem_limit_bytes=size + (4 << 20)
+            collective_id=0, has_side_effects=True, vmem_limit_bytes=min(size + (12 << 20), 60 << 20)
         ),
         name="twins",
     )(view_a, view_b)

time: 181 us -> 166 us (0.917)
  Pallas kernels: 173 us -> 156 us
    pallas_call x1, Pallas kernels: 173 us -> 156 us  [shards(): pl.pallas_call(functools.partial(body, n_row, n_col, width), out_shape=(j...]
where the time goes in v2:
time: 166 us
  Pallas kernels  156 us (94%)
  other arithmetic  5.39 us (3%)
  local copies, waits for them, and re-layouts  3.32 us (2%)
    pallas_call x1, Pallas kernels, shards(): pl.pallas_call(functools.partial(body, n_row, n_col, width), out_shape=(j...  156 us
    div x1, other arithmetic, shards(): return (product / count, loss[0, 0])  5.39 us

profile of v2, /device:TPU:0, one launch (start us, length us, event | category | flops | bytes accessed | tf_op | source)
XLA Modules:
  0.0 165.6 jit_solution(6005115078218351541)
XLA Ops:
  0.6 0.0 copy-start
  0.6 1.4 copy-done
  2.0 0.0 copy-start.1
  2.0 1.4 copy-done.1
  3.4 156.2 %twins.1 = (f32[2048,1024]{1,0:T(8,128)S(1)}, f32[8,128]{1,0:T(8,128)S(1)}) custom-call(bf16[96,8192]{1,0:T(8,128)(2,1)S(1)} %copy-done, bf16[96,8192]{1,0:T(8,128)(2,1)S(1)} %copy-done.1), custom_call_target="tpu_custom_call" | custom-call | tf_op jit(solution)/shard_map/twins/pallas_call | solution.py:412
  159.6 0.5 slice.3
  160.2 5.4 %broadcast_multiply_fusion = f32[2048,1024]{1,0:T(8,128)} fusion(f32[2048,1024]{1,0:T(8,128)S(1)} %get-tuple-element.4), kind=kLoop, calls=%fused_computation | loop fusion | flops 2097152 | bytes 16777216 | tf_op jit(solution)/shard_map/div | solution.py:445
Async XLA Ops:
  0.6 1.4 copy-start
  2.0 1.4 copy-start.1

commit v3 on v2

--- a/solution.py
+++ b/solution.py
@@ -239,30 +239,36 @@
     coefs(stat_b, coef_b)
 
     tile = min(1024, rb)
-    depth = 2 * n_row * t
-
-    def process(zz):
-        pair = pl.ds(zz * 2, 2)
-        for p in range(n_row):
-            across(zz * 2 + (1 - k), p).wait_recv()
+
+    def wait_fwd(zz):
         for g in range(2):
             for i in range(1, n_row):
                 got_fwd(i, zz * 2 + g).wait_recv()
 
+    def process(zz):
+        for p in range(n_row):
+            across(zz * 2 + (1 - k), p).wait_recv()
+        wait_fwd(zz)
+        multiply(zz, pl.ds(0, n_row * t), n_row * t)
+
+    def multiply(zz, rows, height):
+        pair = pl.ds(zz * 2, 2)
+        depth = 2 * height
+
         def norm_b(q, carry):
             cols = pl.ds(pl.multiple_of(q * 128, 128), 128)
-            x = b_all[pair, :, cols].astype(F32).reshape(depth, 128)
-            nb[:, cols] = ((x - coef_b[0:1, cols]) * coef_b[1:2, cols]).astype(BF16)
+            x = b_all[pair, rows, cols].astype(F32).reshape(depth, 128)
+            nb[0:depth, cols] = ((x - coef_b[0:1, cols]) * coef_b[1:2, cols]).astype(BF16)
             return carry
 
         lax.fori_loop(0, cb // 128, norm_b, 0)
 
         def mul(q, carry):
             cols = pl.ds(pl.multiple_of(q * tile, tile), tile)
-            x = a_all[pair, :, cols].astype(F32).reshape(depth, tile)
+            x = a_all[pair, rows, cols].astype(F32).reshape(depth, tile)
             na = ((x - coef_a[0:1, cols]) * coef_a[1:2, cols]).astype(BF16)
             out[cols, :] += lax.dot_general(
-                na, nb[...], (((0,), (0,)), ((), ())), preferred_element_type=F32
+                na, nb[0:depth, :], (((0,), (0,)), ((), ())), preferred_element_type=F32
             )
             return carry
 
@@ -310,6 +316,24 @@
 
                 across(high, p).start()
 
+    def last():
+        zz = jnp.where(z == 0, n_z - 1, 0)
+        g = zz * 2 + k
+
+        @pl.when(jnp.logical_or(z == 0, z == n_z - 1))
+        def _():
+            wait_fwd(zz)
+
+            def one(o, carry):
+                p = slice_at(o)
+                up(g, p).wait_recv()
+                across(g, p).start()
+                across(zz * 2 + (1 - k), p).wait_recv()
+                multiply(zz, pl.ds(pl.multiple_of(p * t, t), t), t)
+                return carry
+
+            lax.fori_loop(0, n_row, one, 0)
+
     def step(d, carry):
         @pl.when(d + 1 < n_z - 1)
         def _():
@@ -317,13 +341,11 @@
 
         process_all(d)
 
-        @pl.when(d + 1 == n_z - 1)
-        def _():
-            relay(d + 1)
-
-        return carry
-
-    lax.fori_loop(0, n_z, step, 0)
+        return carry
+
+    lax.fori_loop(0, max(n_z - 1, 1), step, 0)
+    if n_z > 1:
+        last()
 
     def part(q, carry):
         rows = pl.ds(pl.multiple_of(q * 8, 8), 8)

time: 166 us -> 163 us (0.982)
  Pallas kernels: 156 us -> 154 us
    pallas_call x1, Pallas kernels: 156 us -> 154 us  [shards(): pl.pallas_call(functools.partial(body, n_row, n_col, width), out_shape=(j...]
where the time goes in v3:
time: 163 us
  Pallas kernels  154 us (94%)
  other arithmetic  5.39 us (3%)
  local copies, waits for them, and re-layouts  3.32 us (2%)
    pallas_call x1, Pallas kernels, shards(): pl.pallas_call(functools.partial(body, n_row, n_col, width), out_shape=(j...  154 us
    div x1, other arithmetic, shards(): return (product / count, loss[0, 0])  5.39 us

profile of v3, /device:TPU:0, one launch (start us, length us, event | category | flops | bytes accessed | tf_op | source)
XLA Modules:
  0.0 163.1 jit_solution(10926305067698497681)
XLA Ops:
  0.6 0.0 copy-start
  0.6 1.4 copy-done
  2.0 0.0 copy-start.1
  2.0 1.4 copy-done.1
  3.4 153.7 %twins.1 = (f32[2048,1024]{1,0:T(8,128)S(1)}, f32[8,128]{1,0:T(8,128)S(1)}) custom-call(bf16[96,8192]{1,0:T(8,128)(2,1)S(1)} %copy-done, bf16[96,8192]{1,0:T(8,128)(2,1)S(1)} %copy-done.1), custom_call_target="tpu_custom_call" | custom-call | tf_op jit(solution)/shard_map/twins/pallas_call | solution.py:434
  157.2 0.5 slice.3
  157.7 5.4 %broadcast_multiply_fusion = f32[2048,1024]{1,0:T(8,128)} fusion(f32[2048,1024]{1,0:T(8,128)S(1)} %get-tuple-element.4), kind=kLoop, calls=%fused_computation | loop fusion | flops 2097152 | bytes 16777216 | tf_op jit(solution)/shard_map/div | solution.py:467
Async XLA Ops:
  0.6 1.4 copy-start
  2.0 1.4 copy-start.1
